TPU v7x, 32 devices: a 4x4x1 block of a 4x4x8 slice. The times are simulated.
32 devices in a mesh: rep: 1 (over z), dp: 32 (over x, y, core).
Axes of the slice: x: 4, y: 4, z: 1, core: 2. Of those that a mesh axis runs over, the one named last changes fastest.
The devices are a block of a 4x4x8 slice.
Arguments:
- a: bfloat16 [32, 2, 4096, 1024], P(('rep', 'dp'))
- g: bfloat16 [32, 2, 4096, 2560], P(('rep', 'dp'))
Outputs:
- output: bfloat16 [2, 1024, 2560], P('rep')
All inputs are finite; a program needn't handle non-finite values.
Results may differ from a plain program's by a relative error of at most 0.012.
Values are sent between devices in bfloat16 or wider.
A program may use at most 768 MiB of HBM per device.

v0:
```python
import jax
import jax.numpy as jnp


def solution(mesh):
    groups = mesh.shape["rep"]

    def step(a, g):
        a, g = (t.reshape(groups, -1, *t.shape[1:]) for t in (a, g))
        sums = jnp.einsum("rsntd,rsntf->rndf", a, g, preferred_element_type=jnp.float32)
        return sums.astype(jnp.bfloat16).reshape(-1, *sums.shape[2:])

    return step
```

profile of v0, /device:TPU:97, one launch (start us, length us, event | category | flops | bytes accessed | tf_op | source)
XLA Modules:
  0.0 207.3 jit_solution(14606717158293496086)
XLA Ops:
  0.0 52.4 %fusion = f32[2,1024,2560]{2,1,0:T(8,128)} fusion(bf16[1,2,4096,2560]{3,2,1,0:T(8,128)(2,1)} %param.1, bf16[1,2,4096,1024]{3,2,1,0:T(8,128)(2,1)} %param), kind=kOutput, calls=%fused_computation | convolution fusion | flops 42949672960 | bytes 79691776 | tf_op jit(solution)/rsntd,rsntf->rndf/dot_general | solution.py:10
  52.4 154.9 %all-reduce.2 = bf16[2,1024,2560]{2,1,0:T(8,128)(2,1)} all-reduce(f32[2,1024,2560]{2,1,0:T(8,128)} %fusion), channel_id=1, replica_groups=mesh['axis_0'=32] {'axis_0'}, use_global_device_ids=true, to_apply=%add.clone | all-reduce | flops 5242880 | bytes 31457280 | tf_op jit(solution)/rsntd,rsntf->rndf/dot_general | solution.py:10
where the time goes:
time: 207 us
  blocking collectives  155 us (75%)
  matrix products  52.4 us (25%)
    dot_general x1, blocking collectives, step(): jnp.einsum('rsntd,rsntf->rndf', a, g, preferred_element_type=jnp.float32)  155 us
    dot_general x1, matrix products, step(): jnp.einsum('rsntd,rsntf->rndf', a, g, preferred_element_type=jnp.float32)  52.4 us

commit v1 on v0

v1 whole, which is shorter than its diff:
```python
import functools
import math

import jax
import jax.numpy as jnp
from jax import lax
from jax.experimental import pallas as pl
from jax.experimental.pallas import tpu as pltpu
from jax.sharding import PartitionSpec as P

CORES = 2
RING = 4
SLOTS = 3
MESSAGES = 25
MESH = pl.DeviceIdType.MESH


def kernel(
    pieces, width, a_hbm, g_hbm, out_hbm,
    a_buf, g_buf, own, pair_send, pair_recv, raw, mid1, sum1, mid2, recv1, recv2, res,
    a_sem, g_sem, out_sem, send_sem, recv_sem,
):
    matrices, tokens, d = a_hbm.shape[1:]
    half = d // CORES
    block = half // RING
    cell = block // RING
    per_matrix = pieces // matrices

    me = lax.axis_index("dp")
    core = lax.rem(me, CORES)
    chip = me // CORES
    x, y = chip // RING, lax.rem(chip, RING)
    other = 1 - core
    p1 = x * other + y * core
    p2 = y * other + x * core

    def at(q1, q2):
        return ((q1 * other + q2 * core) * RING + q2 * other + q1 * core) * CORES + core

    def step(p, by):
        return lax.rem(p + by + RING, RING)

    partner = chip * CORES + other
    right1, left1 = at(step(p1, 1), p2), at(step(p1, -1), p2)
    right2, left2 = at(p1, step(p2, 1)), at(p1, step(p2, -1))
    peers = (partner, right1, left1, right2, left2)

    def rows(start, size):
        return pl.ds(pl.multiple_of(start, size), size)

    def copy(j, message, src, dst, device):
        return pltpu.make_async_remote_copy(
            src_ref=src, dst_ref=dst, send_sem=send_sem.at[j, message], recv_sem=recv_sem.at[j, message],
            device_id={"dp": device}, device_id_type=MESH,
        )

    def send(j, message, src, dst, device):
        copy(j, message, src, dst, device).start()

    def sent(j, message, src):
        copy(j, message, src, src, partner).wait_send()

    def got(j, message, dst):
        copy(j, message, dst, dst, partner).wait_recv()

    def load_a(n, h):
        start = (core * h + other * (1 - h)) * half
        return pltpu.make_async_copy(
            a_hbm.at[0, n, :, pl.ds(pl.multiple_of(start, half), half)], a_buf.at[n, h], a_sem.at[n, h]
        )

    def load_g(j):
        n, c = j // per_matrix, lax.rem(j, per_matrix)
        s = lax.rem(j, SLOTS)
        return pltpu.make_async_copy(
            g_hbm.at[0, n, :, pl.ds(pl.multiple_of(c * width, width), width)], g_buf.at[s], g_sem.at[j]
        )

    def store_out(j):
        n, c = j // per_matrix, lax.rem(j, per_matrix)
        return pltpu.make_async_copy(
            res.at[j], out_hbm.at[n, :, pl.ds(pl.multiple_of(c * width, width), width)], out_sem.at[j]
        )

    def dot(j, h):
        n, s = j // per_matrix, lax.rem(j, SLOTS)
        return lax.dot_general(
            a_buf[n, h], g_buf[s], (((0,), (0,)), ((), ())), preferred_element_type=jnp.float32
        )

    load_a(0, 0).start()
    load_g(0).start()
    load_a(0, 1).start()
    load_g(1).start()
    load_g(2).start()
    for n in range(1, matrices):
        for h in range(2):
            load_a(n, h).start()

    barrier = pltpu.get_barrier_semaphore()
    for peer in peers:
        pl.semaphore_signal(barrier, inc=1, device_id={"dp": peer}, device_id_type=MESH)
    pl.semaphore_wait(barrier, len(peers))

    def partner_half(j):
        load_g(j).wait()

        @pl.when(lax.rem(j, per_matrix) == 0)
        def _():
            load_a(j // per_matrix, 0).wait()

        s = lax.rem(j, 2)
        pair_send[s] = dot(j, 0).astype(jnp.bfloat16)
        send(j, 0, pair_send.at[s], pair_recv.at[j], partner)

    def own_half(j):
        @pl.when(lax.rem(j, per_matrix) == 0)
        def _():
            load_a(j // per_matrix, 1).wait()

        s = lax.rem(j, SLOTS)
        got(j, 0, pair_recv.at[j])
        total = dot(j, 1) + pair_recv[j].astype(jnp.float32)
        own[s] = total
        raw[s] = total.astype(jnp.bfloat16)

        @pl.when(j + SLOTS < pieces)
        def _():
            load_g(j + SLOTS).start()

        scatter_raw(j, 1, raw.at[s], recv1.at[j], p1, block, right1, left1)
        sent(j, 0, pair_send.at[lax.rem(j, 2)])

    def scatter_raw(j, first, src, dst, p, size, right, left):
        h = size // 2
        far, near_r, near_l = step(p, 2) * size, step(p, 1) * size, step(p, -1) * size
        send(j, first, src.at[rows(far, h)], dst.at[0], right)
        send(j, first + 1, src.at[rows(far + h, h)], dst.at[1], left)
        send(j, first + 2, src.at[rows(near_r + h, h)], dst.at[2], right)
        send(j, first + 3, src.at[rows(near_l, h)], dst.at[3], left)

    def scatter_mid(j, first, acc, stage, dst, p, size, right, left):
        h = size // 2
        near_r, near_l = step(p, 1) * size, step(p, -1) * size
        got(j, first, dst.at[0])
        stage[0] = (acc[rows(near_r, h)] + dst[0].astype(jnp.float32)).astype(jnp.bfloat16)
        send(j, first + 4, stage.at[0], dst.at[4], right)
        got(j, first + 1, dst.at[1])
        stage[1] = (acc[rows(near_l + h, h)] + dst[1].astype(jnp.float32)).astype(jnp.bfloat16)
        send(j, first + 5, stage.at[1], dst.at[5], left)

    def scatter_sum(j, first, acc, dst, p, size):
        h = size // 2
        for m in (2, 3, 4, 5):
            got(j, first + m, dst.at[m])
        upper = acc[rows(p * size, h)] + (dst[3].astype(jnp.float32) + dst[4].astype(jnp.float32))
        lower = acc[rows(p * size + h, h)] + (dst[2].astype(jnp.float32) + dst[5].astype(jnp.float32))
        return upper, lower

    def scatter_sent(j, first, src, stage, size):
        h = size // 2
        for m in range(4):
            sent(j, first + m, src.at[pl.ds(0, h)])
        for m in range(2):
            sent(j, first + 4 + m, stage.at[m])

    def mid_1(j):
        s = lax.rem(j, SLOTS)
        scatter_mid(j, 1, own.at[s], mid1.at[s], recv1.at[j], p1, block, right1, left1)

    def sum_1(j):
        s = lax.rem(j, SLOTS)
        h = block // 2
        for part, value in enumerate(scatter_sum(j, 1, own.at[s], recv1.at[j], p1, block)):
            own[s, pl.ds(part * h, h)] = value
            sum1[s, pl.ds(part * h, h)] = value.astype(jnp.bfloat16)
        scatter_raw(j, 7, sum1.at[s], recv2.at[j], p2, cell, right2, left2)

    def mid_2(j):
        s = lax.rem(j, SLOTS)
        scatter_mid(j, 7, own.at[s], mid2.at[s], recv2.at[j], p2, cell, right2, left2)

    def cells(q1, q2):
        return core * half + q1 * block + q2 * cell

    def sum_2(j):
        s = lax.rem(j, SLOTS)
        h = cell // 2
        for part, value in enumerate(scatter_sum(j, 7, own.at[s], recv2.at[j], p2, cell)):
            res[j, rows(cells(p1, p2) + part * h, h)] = value.astype(jnp.bfloat16)
        mine = res.at[j, rows(cells(p1, p2), cell)]
        send(j, 13, mine, mine, right2)
        send(j, 14, mine, mine, left2)

    def piece_rows(j, start, size):
        return res.at[j, rows(start, size)]

    def gather_mid_2(j):
        h = cell // 2
        got(j, 13, piece_rows(j, cells(p1, step(p2, -1)), cell))
        ref = piece_rows(j, cells(p1, step(p2, -1)), h)
        send(j, 15, ref, ref, right2)
        got(j, 14, piece_rows(j, cells(p1, step(p2, 1)), cell))
        ref = piece_rows(j, cells(p1, step(p2, 1)) + h, h)
        send(j, 16, ref, ref, left2)
        scatter_sent(j, 1, raw.at[0], mid1.at[0], block)

    def gather_1(j):
        h = cell // 2
        got(j, 15, piece_rows(j, cells(p1, step(p2, 2)), h))
        got(j, 16, piece_rows(j, cells(p1, step(p2, 2)) + h, h))
        mine = piece_rows(j, cells(p1, 0), block)
        send(j, 17, mine, mine, right1)
        send(j, 18, mine, mine, left1)
        send(j, 21, mine, mine, partner)

    def gather_mid_1(j):
        h = block // 2
        from_left, from_right = cells(step(p1, -1), 0), cells(step(p1, 1), 0)
        got(j, 17, piece_rows(j, from_left, block))
        ref = piece_rows(j, from_left, h)
        send(j, 19, ref, ref, right1)
        got(j, 18, piece_rows(j, from_right, block))
        ref = piece_rows(j, from_right + h, h)
        send(j, 20, ref, ref, left1)
        for message, start in ((22, from_left), (23, from_right)):
            ref = piece_rows(j, start, block)
            send(j, message, ref, ref, partner)
        scatter_sent(j, 7, sum1.at[0], mid2.at[0], cell)

    def gather_end(j):
        h = block // 2
        far = cells(step(p1, 2), 0)
        got(j, 19, piece_rows(j, far, h))
        got(j, 20, piece_rows(j, far + h, h))
        ref = piece_rows(j, far, block)
        send(j, 24, ref, ref, partner)

    def finish(j):
        for message in (13, 14):
            sent(j, message, res.at[j, pl.ds(0, cell)])
        for message in (15, 16):
            sent(j, message, res.at[j, pl.ds(0, cell // 2)])
        for message in (17, 18, 21, 22, 23, 24):
            sent(j, message, res.at[j, pl.ds(0, block)])
        for message in (19, 20):
            sent(j, message, res.at[j, pl.ds(0, block // 2)])
        theirs = other * half
        for message, by in ((21, 0), (22, -1), (23, 1), (24, 2)):
            got(j, message, piece_rows(j, theirs + step(p2, by) * block, block))
        store_out(j).start()

    def when_piece(j, stage):
        @pl.when((j >= 0) & (j < pieces))
        def _():
            stage(j)

    def body(i, _):
        when_piece(i, partner_half)
        when_piece(i - 6, finish)
        when_piece(i - 5, gather_mid_1)
        when_piece(i - 4, gather_mid_2)
        when_piece(i - 3, mid_2)
        when_piece(i - 2, mid_1)
        when_piece(i - 1, own_half)
        when_piece(i - 5, gather_end)
        when_piece(i - 4, gather_1)
        when_piece(i - 3, sum_2)
        when_piece(i - 2, sum_1)
        return 0

    lax.fori_loop(0, pieces + 7, body, 0)
    lax.fori_loop(0, pieces, lambda j, _: (store_out(j).wait(), 0)[1], 0)


def solution(mesh):
    devices = mesh.shape["dp"]
    assert devices == CORES * RING * RING and RING == math.isqrt(devices // CORES)

    def sums(a, g):
        _, matrices, tokens, d = a.shape
        ff = g.shape[3]
        width = 512 if ff % 512 == 0 else 128
        pieces = matrices * ff // width
        half = d // CORES
        block, cell = half // RING, half // RING // RING
        bf16, f32 = jnp.bfloat16, jnp.float32
        return pl.pallas_call(
            functools.partial(kernel, pieces, width),
            out_shape=jax.ShapeDtypeStruct((matrices, d, ff), bf16),
            in_specs=[pl.BlockSpec(memory_space=pltpu.HBM)] * 2,
            out_specs=pl.BlockSpec(memory_space=pltpu.HBM),
            scratch_shapes=[
                pltpu.VMEM((matrices, 2, tokens, half), bf16),
                pltpu.VMEM((SLOTS, tokens, width), bf16),
                pltpu.VMEM((SLOTS, half, width), f32),
                pltpu.VMEM((2, half, width), bf16),
                pltpu.VMEM((pieces, half, width), bf16),
                pltpu.VMEM((SLOTS, half, width), bf16),
                pltpu.VMEM((SLOTS, 2, block // 2, width), bf16),
                pltpu.VMEM((SLOTS, block, width), bf16),
                pltpu.VMEM((SLOTS, 2, cell // 2, width), bf16),
                pltpu.VMEM((pieces, 6, block // 2, width), bf16),
                pltpu.VMEM((pieces, 6, cell // 2, width), bf16),
                pltpu.VMEM((pieces, d, width), bf16),
                pltpu.SemaphoreType.DMA((matrices, 2)),
                pltpu.SemaphoreType.DMA((pieces,)),
                pltpu.SemaphoreType.DMA((pieces,)),
                pltpu.SemaphoreType.DMA((pieces, MESSAGES)),
                pltpu.SemaphoreType.DMA((pieces, MESSAGES)),
            ],
            compiler_params=pltpu.CompilerParams(
                collective_id=0, has_side_effects=True, vmem_limit_bytes=63 * 2**20
            ),
        )(a, g)

    spec = P(("rep", "dp"))
    return jax.shard_map(sums, mesh=mesh, in_specs=(spec, spec), out_specs=P("rep"), check_vma=False)
```

time: 207 us -> 143 us (0.69)
  blocking collectives: 155 us -> 0 us
  Pallas kernels: 0 us -> 134 us
  matrix products: 52.4 us -> 0 us
  local copies, waits for them, and re-layouts: 0 us -> 8.74 us
    dot_general x1 -> x0, blocking collectives: 155 us -> none  [step(): jnp.einsum('rsntd,rsntf->rndf', a, g, preferred_element_type=jnp.float32)]
    pallas_call x0 -> x1, Pallas kernels: none -> 134 us  [sums(): pl.pallas_call(functools.partial(kernel, pieces, width), out_shape=jax.Sh...]
    dot_general x1 -> x0, matrix products: 52.4 us -> none  [step(): jnp.einsum('rsntd,rsntf->rndf', a, g, preferred_element_type=jnp.float32)]
    unnamed x0 -> x1, local copies, waits for them, and re-layouts: none -> 8.74 us
where the time goes in v1:
time: 143 us
  Pallas kernels  134 us (94%)
  local copies, waits for them, and re-layouts  8.74 us (6%)
    pallas_call x1, Pallas kernels, sums(): pl.pallas_call(functools.partial(kernel, pieces, width), out_shape=jax.Sh...  134 us
    unnamed x1, local copies, waits for them, and re-layouts  8.74 us

profile of v1, /device:TPU:97, one launch (start us, length us, event | category | flops | bytes accessed | tf_op | source)
XLA Modules:
  0.0 142.6 jit_solution(16735102409848959380)
XLA Ops:
  0.0 133.8 %shard_map.28 = bf16[2,1024,2560]{2,1,0:T(8,128)(2,1)} custom-call(bf16[1,2,4096,1024]{3,2,1,0:T(8,128)(2,1)} %a_hbm.1, bf16[1,2,4096,2560]{3,2,1,0:T(8,128)(2,1)} %g_hbm.1), custom_call_target="tpu_custom_call" | custom-call | tf_op jit(solution)/shard_map/pallas_call | solution.py:288
  133.8 8.7 %copy.4 = bf16[2,1024,2560]{2,1,0:T(8,128)(2,1)} copy(bf16[2,1024,2560]{2,1,0:T(8,128)(2,1)} %shard_map.28) | data formatting | bytes 20971520

commit v2 on v1

v2 whole, which is shorter than its diff:
```python
import functools
import math

import jax
import jax.numpy as jnp
from jax import lax
from jax.experimental import pallas as pl
from jax.experimental.pallas import tpu as pltpu
from jax.sharding import PartitionSpec as P

CORES = 2
RING = 4
MESSAGES = 25
VMEM_BYTES = 52 * 2**20
MESH = pl.DeviceIdType.MESH

DIRECT_FIRST, DIRECT_LAST = 2, 2
DIRECT = {"own_half": 3, "sum_1": 6, "sum_2": 8, "gather_1": 11, "gather_mid_1": 15, "gather_end": 16, "finish": 19}
PASSED = {"own_half": 3, "mid_1": 5, "sum_1": 8, "sum_2": 11, "gather_1": 14, "gather_mid_1": 16, "gather_end": 20, "finish": 23}


def slots(written, read):
    whens = [when for when in (DIRECT, PASSED) if written in when]
    return max((late[read] - early[written]) // 2 + 1 for late in whens for early in whens)


G_SLOTS = 3
OWN_SLOTS = slots("own_half", "sum_2")
RAW_SLOTS = slots("own_half", "sum_1")
MID_SLOTS = slots("mid_1", "sum_1")
SUM_SLOTS = slots("sum_1", "sum_2")


def kernel(
    pieces, width, a_hbm, g_hbm, res,
    a_buf, g_buf, own, pair_send, pair_recv, raw, mid1, sum1, recv1, recv2,
    a_sem, g_sem, send_sem, recv_sem,
):
    matrices, tokens, d = a_hbm.shape[1:]
    half = d // CORES
    block = half // RING
    cell = block // RING
    per_matrix = pieces // matrices

    me = lax.axis_index("dp")
    core = lax.rem(me, CORES)
    chip = me // CORES
    x, y = chip // RING, lax.rem(chip, RING)
    other = 1 - core
    p1 = x * other + y * core
    p2 = y * other + x * core

    def at(q1, q2):
        return ((q1 * other + q2 * core) * RING + q2 * other + q1 * core) * CORES + core

    def step(p, by):
        return lax.rem(p + by + RING, RING)

    partner = chip * CORES + other
    right1, left1, far1 = (at(step(p1, by), p2) for by in (1, -1, 2))
    right2, left2, far2 = (at(p1, step(p2, by)) for by in (1, -1, 2))
    peers = (partner, right1, left1, far1, right2, left2, far2)

    def rows(start, size):
        return pl.ds(pl.multiple_of(start, size), size)

    def copy(j, message, src, dst, device):
        return pltpu.make_async_remote_copy(
            src_ref=src, dst_ref=dst, send_sem=send_sem.at[j, message], recv_sem=recv_sem.at[j, message],
            device_id={"dp": device}, device_id_type=MESH,
        )

    def send(j, message, src, dst, device):
        copy(j, message, src, dst, device).start()

    def sent(j, message, src):
        copy(j, message, src, src, partner).wait_send()

    def got(j, message, dst):
        copy(j, message, dst, dst, partner).wait_recv()

    def load_a(n, h):
        start = (core * h + other * (1 - h)) * half
        return pltpu.make_async_copy(
            a_hbm.at[0, n, :, pl.ds(pl.multiple_of(start, half), half)], a_buf.at[n, h], a_sem.at[n, h]
        )

    def load_g(j):
        n, c = j // per_matrix, lax.rem(j, per_matrix)
        s = lax.rem(j, G_SLOTS)
        return pltpu.make_async_copy(
            g_hbm.at[0, n, :, pl.ds(pl.multiple_of(c * width, width), width)], g_buf.at[s], g_sem.at[j]
        )

    def dot(j, h):
        n, s = j // per_matrix, lax.rem(j, G_SLOTS)
        return lax.dot_general(
            a_buf[n, h], g_buf[s], (((0,), (0,)), ((), ())), preferred_element_type=jnp.float32
        )

    barrier = pltpu.get_barrier_semaphore()
    load_a(0, 0).start()
    load_g(0).start()
    for peer in peers:
        pl.semaphore_signal(barrier, inc=1, device_id={"dp": peer}, device_id_type=MESH)
    load_a(0, 1).start()
    load_g(1).start()
    load_g(2).start()

    def partner_dot(j):
        pair_send[lax.rem(j, 2)] = dot(j, 0).astype(jnp.bfloat16)

    def partner_send(j):
        send(j, 0, pair_send.at[lax.rem(j, 2)], pair_recv.at[j], partner)

    load_g(0).wait()
    load_a(0, 0).wait()
    partner_dot(0)
    pl.semaphore_wait(barrier, len(peers))
    partner_send(0)

    def partner_half(j):
        load_g(j).wait()

        @pl.when(lax.rem(j, per_matrix) == 0)
        def _():
            load_a(j // per_matrix, 0).wait()

        @pl.when((lax.rem(j, per_matrix) == 1) & (j // per_matrix + 1 < matrices))
        def _():
            for h in range(2):
                load_a(j // per_matrix + 1, h).start()

        partner_dot(j)
        partner_send(j)

    def direct(j):
        return (j < DIRECT_FIRST) | (j >= pieces - DIRECT_LAST)

    def either(j, if_direct, if_passed):
        pl.when(direct(j))(if_direct)
        pl.when(jnp.logical_not(direct(j)))(if_passed)

    def own_half(j):
        @pl.when(lax.rem(j, per_matrix) == 0)
        def _():
            load_a(j // per_matrix, 1).wait()

        s = lax.rem(j, RAW_SLOTS)
        got(j, 0, pair_recv.at[j])
        total = dot(j, 1) + pair_recv[j].astype(jnp.float32)
        own[lax.rem(j, OWN_SLOTS)] = total
        raw[s] = total.astype(jnp.bfloat16)

        @pl.when(j + G_SLOTS < pieces)
        def _():
            load_g(j + G_SLOTS).start()

        src, h = raw.at[s], block // 2
        far, near_r, near_l = (step(p1, by) * block for by in (2, 1, -1))

        def _direct():
            scatter(j, 1, src, recv1, p1, block, far1, right1, left1)

        def _passed():
            send(j, 1, src.at[rows(far, h)], recv1.at[j, pl.ds(0, h)], right1)
            send(j, 2, src.at[rows(far + h, h)], recv1.at[j, pl.ds(h, h)], left1)
            send(j, 3, src.at[rows(near_r + h, h)], recv1.at[j, pl.ds(2 * h, h)], right1)
            send(j, 4, src.at[rows(near_l, h)], recv1.at[j, pl.ds(3 * h, h)], left1)

        either(j, _direct, _passed)
        sent(j, 0, pair_send.at[lax.rem(j, 2)])

    def scatter(j, first, src, dst, p, size, far, right, left):
        for m, (by, device) in enumerate(((2, far), (1, right), (-1, left))):
            send(j, first + m, src.at[rows(step(p, by) * size, size)], dst.at[j, pl.ds(m * size, size)], device)

    def added(j, first, acc, dst, p, size):
        for m in range(3):
            got(j, first + m, dst.at[j, pl.ds(m * size, size)])
        far, left, right = (dst[j, pl.ds(m * size, size)].astype(jnp.float32) for m in range(3))
        return acc[rows(p * size, size)] + (left + right + far)

    def mid_1(j):
        s, h = lax.rem(j, MID_SLOTS), block // 2
        acc = own.at[lax.rem(j, OWN_SLOTS)]
        for m, device, start in ((0, right1, step(p1, 1) * block), (1, left1, step(p1, -1) * block + h)):
            got(j, 1 + m, recv1.at[j, pl.ds(m * h, h)])
            passed = acc[rows(start, h)] + recv1[j, pl.ds(m * h, h)].astype(jnp.float32)
            mid1[s, m] = passed.astype(jnp.bfloat16)
            send(j, 5 + m, mid1.at[s, m], recv1.at[j, pl.ds((4 + m) * h, h)], device)

    def sum_1(j):
        s, h = lax.rem(j, SUM_SLOTS), block // 2
        acc = own.at[lax.rem(j, OWN_SLOTS)]

        def keep(start, value):
            acc[pl.ds(start, value.shape[0])] = value
            sum1[s, pl.ds(start, value.shape[0])] = value.astype(jnp.bfloat16)

        def _direct():
            keep(0, added(j, 1, acc, recv1, p1, block))
            for m in range(3):
                sent(j, 1 + m, raw.at[0, pl.ds(0, block)])

        def _passed():
            for m in range(2, 6):
                got(j, 1 + m, recv1.at[j, pl.ds(m * h, h)])
            part = [recv1[j, pl.ds(m * h, h)].astype(jnp.float32) for m in range(2, 6)]
            upper = acc[rows(p1 * block, h)] + (part[1] + part[2])
            lower = acc[rows(p1 * block + h, h)] + (part[0] + part[3])
            keep(0, upper)
            keep(h, lower)
            for m in range(6):
                sent(j, 1 + m, mid1.at[0, 0])

        either(j, _direct, _passed)
        scatter(j, 7, sum1.at[s], recv2, p2, cell, far2, right2, left2)

    def cells(q1, q2):
        return core * half + q1 * block + q2 * cell

    def piece_rows(j, start, size):
        return res.at[j, rows(start, size)]

    def sum_2(j):
        acc = own.at[lax.rem(j, OWN_SLOTS)]
        res[j, rows(cells(p1, p2), cell)] = added(j, 7, acc, recv2, p2, cell).astype(jnp.bfloat16)
        mine = piece_rows(j, cells(p1, p2), cell)
        for m, device in enumerate((far2, right2, left2)):
            send(j, 13 + m, mine, mine, device)
        for m in range(3):
            sent(j, 7 + m, sum1.at[0, pl.ds(0, cell)])

    def gather_1(j):
        for m, by in enumerate((2, -1, 1)):
            got(j, 13 + m, piece_rows(j, cells(p1, step(p2, by)), cell))
        mine = piece_rows(j, cells(p1, 0), block)

        @pl.when(direct(j))
        def _():
            send(j, 19, mine, mine, far1)

        send(j, 17, mine, mine, right1)
        send(j, 18, mine, mine, left1)
        send(j, 21, mine, mine, partner)

    def gather_mid_1(j):
        h = block // 2
        from_left, from_right = cells(step(p1, -1), 0), cells(step(p1, 1), 0)
        got(j, 17, piece_rows(j, from_left, block))
        got(j, 18, piece_rows(j, from_right, block))

        @pl.when(jnp.logical_not(direct(j)))
        def _():
            upper, lower = piece_rows(j, from_left, h), piece_rows(j, from_right + h, h)
            send(j, 19, upper, upper, right1)
            send(j, 20, lower, lower, left1)

        for message, start in ((22, from_left), (23, from_right)):
            ref = piece_rows(j, start, block)
            send(j, message, ref, ref, partner)

    def gather_end(j):
        h, far = block // 2, cells(step(p1, 2), 0)

        def _passed():
            got(j, 19, piece_rows(j, far, h))
            got(j, 20, piece_rows(j, far + h, h))

        either(j, lambda: got(j, 19, piece_rows(j, far, block)), _passed)
        ref = piece_rows(j, far, block)
        send(j, 24, ref, ref, partner)

    def finish(j):
        whole, part = res.at[j, pl.ds(0, block)], res.at[j, pl.ds(0, block // 2)]
        for m in range(3):
            sent(j, 13 + m, res.at[j, pl.ds(0, cell)])
        for message in (17, 18, 21, 22, 23, 24):
            sent(j, message, whole)

        def _passed():
            sent(j, 19, part)
            sent(j, 20, part)

        either(j, lambda: sent(j, 19, whole), _passed)
        theirs = other * half
        for message, by in ((21, 0), (22, -1), (23, 1), (24, 2)):
            got(j, message, piece_rows(j, theirs + step(p2, by) * block, block))

    stages = {
        "own_half": own_half, "mid_1": mid_1, "sum_1": sum_1, "sum_2": sum_2, "gather_1": gather_1,
        "gather_mid_1": gather_mid_1, "gather_end": gather_end, "finish": finish,
    }

    def body(i, _):
        @pl.when((i >= 1) & (i < pieces))
        def _():
            partner_half(i)

        for part in range(2):
            todo = {}
            for is_direct, when in ((True, DIRECT), (False, PASSED)):
                for name, at_half in when.items():
                    if at_half % 2 == part:
                        todo.setdefault((at_half // 2, name), []).append(is_direct)
            order = sorted(todo, key=lambda k: (k[0], list(stages).index(k[1])))
            for late, name in order:
                j = i - late
                use = (j >= 0) & (j < pieces)
                if len(todo[late, name]) == 1:
                    mode = direct(j) if todo[late, name][0] else jnp.logical_not(direct(j))
                    use = use & mode
                pl.when(use)(functools.partial(stages[name], j))
        return 0

    last = max(max(when.values()) for when in (DIRECT, PASSED))
    lax.fori_loop(0, pieces + last // 2, body, 0)


def lay_out(pieces, width, res, out_hbm, sem):
    per_matrix = pieces // out_hbm.shape[0]
    copies = [
        pltpu.make_async_copy(
            res.at[j], out_hbm.at[j // per_matrix, :, pl.ds(j % per_matrix * width, width)], sem.at[j]
        )
        for j in range(pieces)
    ]
    for copy in copies:
        copy.start()
    for copy in copies:
        copy.wait()


def solution(mesh):
    devices = mesh.shape["dp"]
    assert devices == CORES * RING * RING and RING == math.isqrt(devices // CORES)

    def sums(a, g):
        _, matrices, tokens, d = a.shape
        ff = g.shape[3]
        width = 512 if ff % 512 == 0 else 128
        pieces = matrices * ff // width
        half = d // CORES
        block, cell = half // RING, half // RING // RING
        bf16, f32 = jnp.bfloat16, jnp.float32
        summed = pl.pallas_call(
            functools.partial(kernel, pieces, width),
            out_shape=pltpu.VMEM((pieces, d, width), bf16),
            in_specs=[pl.BlockSpec(memory_space=pltpu.HBM)] * 2,
            out_specs=pl.BlockSpec(memory_space=pltpu.VMEM),
            scratch_shapes=[
                pltpu.VMEM((matrices, 2, tokens, half), bf16),
                pltpu.VMEM((G_SLOTS, tokens, width), bf16),
                pltpu.VMEM((OWN_SLOTS, half, width), f32),
                pltpu.VMEM((2, half, width), bf16),
                pltpu.VMEM((pieces, half, width), bf16),
                pltpu.VMEM((RAW_SLOTS, half, width), bf16),
                pltpu.VMEM((MID_SLOTS, 2, block // 2, width), bf16),
                pltpu.VMEM((SUM_SLOTS, block, width), bf16),
                pltpu.VMEM((pieces, 3 * block, width), bf16),
                pltpu.VMEM((pieces, 3 * cell, width), bf16),
                pltpu.SemaphoreType.DMA((matrices, 2)),
                pltpu.SemaphoreType.DMA((pieces,)),
                pltpu.SemaphoreType.DMA((pieces, MESSAGES)),
                pltpu.SemaphoreType.DMA((pieces, MESSAGES)),
            ],
            compiler_params=pltpu.CompilerParams(
                collective_id=0, has_side_effects=True, vmem_limit_bytes=VMEM_BYTES
            ),
        )(a, g)
        return pl.pallas_call(
            functools.partial(lay_out, pieces, width),
            out_shape=jax.ShapeDtypeStruct((matrices, d, ff), bf16),
            in_specs=[pl.BlockSpec(memory_space=pl.ANY)],
            out_specs=pl.BlockSpec(memory_space=pltpu.HBM),
            scratch_shapes=[pltpu.SemaphoreType.DMA((pieces,))],
            compiler_params=pltpu.CompilerParams(vmem_limit_bytes=2**20),
        )(summed)

    spec = P(("rep", "dp"))
    return jax.shard_map(sums, mesh=mesh, in_specs=(spec, spec), out_specs=P("rep"), check_vma=False)
```

time: 143 us -> 102 us (0.71)
  Pallas kernels: 134 us -> 101 us
  local copies, waits for them, and re-layouts: 8.74 us -> 0 us
    pallas_call x1 -> x2, Pallas kernels: 134 us -> 101 us  [the longest x1 97.5 us: sums(): pl.pallas_call(functools.partial(kernel, pieces, width), out_shape=pltpu....]
    unnamed x1 -> x0, local copies, waits for them, and re-layouts: 8.74 us -> none
where the time goes in v2:
time: 102 us; the launch traced here: 101 us
  Pallas kernels  101 us (99%)
    pallas_call x1, Pallas kernels, sums(): pl.pallas_call(functools.partial(kernel, pieces, width), out_shape=pltpu....  97.5 us
    pallas_call x1, Pallas kernels, sums(): pl.pallas_call(functools.partial(lay_out, pieces, width), out_shape=jax.S...  4.02 us

profile of v2, /device:TPU:97, one launch (start us, length us, event | category | flops | bytes accessed | tf_op | source)
XLA Modules:
  0.0 101.5 jit_solution(11493223811021533255)
XLA Ops:
  0.0 97.5 %shard_map.28.res = bf16[10,1024,512]{2,1,0:T(8,128)(2,1)S(1)} custom-call(bf16[1,2,4096,1024]{3,2,1,0:T(8,128)(2,1)} %a_hbm.1, bf16[1,2,4096,2560]{3,2,1,0:T(8,128)(2,1)} %g_hbm.1), custom_call_target="tpu_custom_call" | custom-call | tf_op jit(solution)/shard_map/pallas_call | solution.py:347
  97.5 4.0 %shard_map.29 = bf16[2,1024,2560]{2,1,0:T(8,128)(2,1)} custom-call(bf16[10,1024,512]{2,1,0:T(8,128)(2,1)S(1)} %shard_map.28.res), custom_call_target="tpu_custom_call" | custom-call | tf_op jit(solution)/shard_map/pallas_call | solution.py:372

commit v3 on v2

--- a/solution.py
+++ b/solution.py
@@ -10,13 +10,14 @@
 
 CORES = 2
 RING = 4
-MESSAGES = 25
+PAIR, UPPER, LOWER, BLOCKS, CELLS, OUT_CELLS, OUT_NEAR, OUT_FAR, HALF = range(9)
 VMEM_BYTES = 52 * 2**20
 MESH = pl.DeviceIdType.MESH
 
 DIRECT_FIRST, DIRECT_LAST = 2, 2
-DIRECT = {"own_half": 3, "sum_1": 6, "sum_2": 8, "gather_1": 11, "gather_mid_1": 15, "gather_end": 16, "finish": 19}
-PASSED = {"own_half": 3, "mid_1": 5, "sum_1": 8, "sum_2": 11, "gather_1": 14, "gather_mid_1": 16, "gather_end": 20, "finish": 23}
+GATHER_FIRST, GATHER_LAST = 2, 2
+DIRECT = {"own_half": 3, "sum_1": 6, "sum_2": 9, "gather_1": 12, "gather_mid_1": 15, "gather_end": 15, "finish": 17}
+PASSED = {"own_half": 3, "mid_1": 5, "sum_1": 8, "sum_2": 11, "gather_1": 14, "gather_mid_1": 17, "gather_end": 20, "finish": 22}
 
 
 def slots(written, read):
@@ -64,20 +65,20 @@
     def rows(start, size):
         return pl.ds(pl.multiple_of(start, size), size)
 
-    def copy(j, message, src, dst, device):
+    def copy(j, leaves, lands, src, dst, device):
         return pltpu.make_async_remote_copy(
-            src_ref=src, dst_ref=dst, send_sem=send_sem.at[j, message], recv_sem=recv_sem.at[j, message],
+            src_ref=src, dst_ref=dst, send_sem=send_sem.at[j, leaves], recv_sem=recv_sem.at[j, lands],
             device_id={"dp": device}, device_id_type=MESH,
         )
 
-    def send(j, message, src, dst, device):
-        copy(j, message, src, dst, device).start()
-
-    def sent(j, message, src):
-        copy(j, message, src, src, partner).wait_send()
-
-    def got(j, message, dst):
-        copy(j, message, dst, dst, partner).wait_recv()
+    def send(j, leaves, lands, src, dst, device):
+        copy(j, leaves, lands, src, dst, device).start()
+
+    def sent(j, leaves, ref):
+        copy(j, leaves, leaves, ref, ref, partner).wait_send()
+
+    def got(j, lands, ref):
+        copy(j, lands, lands, ref, ref, partner).wait_recv()
 
     def load_a(n, h):
         start = (core * h + other * (1 - h)) * half
@@ -111,7 +112,7 @@
         pair_send[lax.rem(j, 2)] = dot(j, 0).astype(jnp.bfloat16)
 
     def partner_send(j):
-        send(j, 0, pair_send.at[lax.rem(j, 2)], pair_recv.at[j], partner)
+        send(j, PAIR, PAIR, pair_send.at[lax.rem(j, 2)], pair_recv.at[j], partner)
 
     load_g(0).wait()
     load_a(0, 0).wait()
@@ -137,9 +138,12 @@
     def direct(j):
         return (j < DIRECT_FIRST) | (j >= pieces - DIRECT_LAST)
 
-    def either(j, if_direct, if_passed):
-        pl.when(direct(j))(if_direct)
-        pl.when(jnp.logical_not(direct(j)))(if_passed)
+    def gathered_direct(j):
+        return (j < GATHER_FIRST) | (j >= pieces - GATHER_LAST)
+
+    def either(which, if_direct, if_passed):
+        pl.when(which)(if_direct)
+        pl.when(jnp.logical_not(which))(if_passed)
 
     def own_half(j):
         @pl.when(lax.rem(j, per_matrix) == 0)
@@ -147,7 +151,7 @@
             load_a(j // per_matrix, 1).wait()
 
         s = lax.rem(j, RAW_SLOTS)
-        got(j, 0, pair_recv.at[j])
+        got(j, PAIR, pair_recv.at[j])
         total = dot(j, 1) + pair_recv[j].astype(jnp.float32)
         own[lax.rem(j, OWN_SLOTS)] = total
         raw[s] = total.astype(jnp.bfloat16)
@@ -160,35 +164,37 @@
         far, near_r, near_l = (step(p1, by) * block for by in (2, 1, -1))
 
         def _direct():
-            scatter(j, 1, src, recv1, p1, block, far1, right1, left1)
+            scatter(j, BLOCKS, src, recv1, p1, block, far1, right1, left1)
 
         def _passed():
-            send(j, 1, src.at[rows(far, h)], recv1.at[j, pl.ds(0, h)], right1)
-            send(j, 2, src.at[rows(far + h, h)], recv1.at[j, pl.ds(h, h)], left1)
-            send(j, 3, src.at[rows(near_r + h, h)], recv1.at[j, pl.ds(2 * h, h)], right1)
-            send(j, 4, src.at[rows(near_l, h)], recv1.at[j, pl.ds(3 * h, h)], left1)
-
-        either(j, _direct, _passed)
-        sent(j, 0, pair_send.at[lax.rem(j, 2)])
-
-    def scatter(j, first, src, dst, p, size, far, right, left):
+            send(j, BLOCKS, UPPER, src.at[rows(far, h)], recv1.at[j, pl.ds(0, h)], right1)
+            send(j, BLOCKS, LOWER, src.at[rows(far + h, h)], recv1.at[j, pl.ds(h, h)], left1)
+            send(j, BLOCKS, BLOCKS, src.at[rows(near_r + h, h)], recv1.at[j, pl.ds(2 * h, h)], right1)
+            send(j, BLOCKS, BLOCKS, src.at[rows(near_l, h)], recv1.at[j, pl.ds(3 * h, h)], left1)
+
+        either(direct(j), _direct, _passed)
+        sent(j, PAIR, pair_send.at[lax.rem(j, 2)])
+
+    def scatter(j, group, src, dst, p, size, far, right, left):
         for m, (by, device) in enumerate(((2, far), (1, right), (-1, left))):
-            send(j, first + m, src.at[rows(step(p, by) * size, size)], dst.at[j, pl.ds(m * size, size)], device)
-
-    def added(j, first, acc, dst, p, size):
-        for m in range(3):
-            got(j, first + m, dst.at[j, pl.ds(m * size, size)])
+            part = src.at[rows(step(p, by) * size, size)]
+            send(j, group, group, part, dst.at[j, pl.ds(m * size, size)], device)
+
+    def added(j, group, acc, dst, p, size):
+        got(j, group, dst.at[j])
         far, left, right = (dst[j, pl.ds(m * size, size)].astype(jnp.float32) for m in range(3))
         return acc[rows(p * size, size)] + (left + right + far)
 
     def mid_1(j):
         s, h = lax.rem(j, MID_SLOTS), block // 2
         acc = own.at[lax.rem(j, OWN_SLOTS)]
-        for m, device, start in ((0, right1, step(p1, 1) * block), (1, left1, step(p1, -1) * block + h)):
-            got(j, 1 + m, recv1.at[j, pl.ds(m * h, h)])
+        for m, lands, device, start in (
+            (0, UPPER, right1, step(p1, 1) * block), (1, LOWER, left1, step(p1, -1) * block + h)
+        ):
+            got(j, lands, recv1.at[j, pl.ds(m * h, h)])
             passed = acc[rows(start, h)] + recv1[j, pl.ds(m * h, h)].astype(jnp.float32)
             mid1[s, m] = passed.astype(jnp.bfloat16)
-            send(j, 5 + m, mid1.at[s, m], recv1.at[j, pl.ds((4 + m) * h, h)], device)
+            send(j, BLOCKS, BLOCKS, mid1.at[s, m], recv1.at[j, pl.ds((4 + m) * h, h)], device)
 
     def sum_1(j):
         s, h = lax.rem(j, SUM_SLOTS), block // 2
@@ -199,23 +205,19 @@
             sum1[s, pl.ds(start, value.shape[0])] = value.astype(jnp.bfloat16)
 
         def _direct():
-            keep(0, added(j, 1, acc, recv1, p1, block))
-            for m in range(3):
-                sent(j, 1 + m, raw.at[0, pl.ds(0, block)])
+            keep(0, added(j, BLOCKS, acc, recv1, p1, block))
 
         def _passed():
-            for m in range(2, 6):
-                got(j, 1 + m, recv1.at[j, pl.ds(m * h, h)])
+            got(j, BLOCKS, recv1.at[j, pl.ds(2 * h, 4 * h)])
             part = [recv1[j, pl.ds(m * h, h)].astype(jnp.float32) for m in range(2, 6)]
             upper = acc[rows(p1 * block, h)] + (part[1] + part[2])
             lower = acc[rows(p1 * block + h, h)] + (part[0] + part[3])
             keep(0, upper)
             keep(h, lower)
-            for m in range(6):
-                sent(j, 1 + m, mid1.at[0, 0])
-
-        either(j, _direct, _passed)
-        scatter(j, 7, sum1.at[s], recv2, p2, cell, far2, right2, left2)
+
+        either(direct(j), _direct, _passed)
+        scatter(j, CELLS, sum1.at[s], recv2, p2, cell, far2, right2, left2)
+        sent(j, BLOCKS, recv1.at[j])
 
     def cells(q1, q2):
         return core * half + q1 * block + q2 * cell
@@ -225,68 +227,42 @@
 
     def sum_2(j):
         acc = own.at[lax.rem(j, OWN_SLOTS)]
-        res[j, rows(cells(p1, p2), cell)] = added(j, 7, acc, recv2, p2, cell).astype(jnp.bfloat16)
+        res[j, rows(cells(p1, p2), cell)] = added(j, CELLS, acc, recv2, p2, cell).astype(jnp.bfloat16)
         mine = piece_rows(j, cells(p1, p2), cell)
-        for m, device in enumerate((far2, right2, left2)):
-            send(j, 13 + m, mine, mine, device)
-        for m in range(3):
-            sent(j, 7 + m, sum1.at[0, pl.ds(0, cell)])
+        for device in (far2, right2, left2):
+            send(j, HALF, OUT_CELLS, mine, mine, device)
+        sent(j, CELLS, recv2.at[j])
 
     def gather_1(j):
-        for m, by in enumerate((2, -1, 1)):
-            got(j, 13 + m, piece_rows(j, cells(p1, step(p2, by)), cell))
+        got(j, OUT_CELLS, res.at[j, pl.ds(0, 3 * cell)])
         mine = piece_rows(j, cells(p1, 0), block)
 
-        @pl.when(direct(j))
-        def _():
-            send(j, 19, mine, mine, far1)
-
-        send(j, 17, mine, mine, right1)
-        send(j, 18, mine, mine, left1)
-        send(j, 21, mine, mine, partner)
+        @pl.when(gathered_direct(j))
+        def _():
+            send(j, HALF, OUT_FAR, mine, mine, far1)
+
+        send(j, HALF, OUT_NEAR, mine, mine, right1)
+        send(j, HALF, OUT_NEAR, mine, mine, left1)
 
     def gather_mid_1(j):
         h = block // 2
-        from_left, from_right = cells(step(p1, -1), 0), cells(step(p1, 1), 0)
-        got(j, 17, piece_rows(j, from_left, block))
-        got(j, 18, piece_rows(j, from_right, block))
-
-        @pl.when(jnp.logical_not(direct(j)))
-        def _():
-            upper, lower = piece_rows(j, from_left, h), piece_rows(j, from_right + h, h)
-            send(j, 19, upper, upper, right1)
-            send(j, 20, lower, lower, left1)
-
-        for message, start in ((22, from_left), (23, from_right)):
-            ref = piece_rows(j, start, block)
-            send(j, message, ref, ref, partner)
+        got(j, OUT_NEAR, res.at[j, pl.ds(0, 2 * block)])
+
+        @pl.when(jnp.logical_not(gathered_direct(j)))
+        def _():
+            upper = piece_rows(j, cells(step(p1, -1), 0), h)
+            lower = piece_rows(j, cells(step(p1, 1), 0) + h, h)
+            send(j, HALF, OUT_FAR, upper, upper, right1)
+            send(j, HALF, OUT_FAR, lower, lower, left1)
 
     def gather_end(j):
-        h, far = block // 2, cells(step(p1, 2), 0)
-
-        def _passed():
-            got(j, 19, piece_rows(j, far, h))
-            got(j, 20, piece_rows(j, far + h, h))
-
-        either(j, lambda: got(j, 19, piece_rows(j, far, block)), _passed)
-        ref = piece_rows(j, far, block)
-        send(j, 24, ref, ref, partner)
+        got(j, OUT_FAR, res.at[j, pl.ds(0, block)])
+        ours = piece_rows(j, core * half, half)
+        send(j, HALF, HALF, ours, ours, partner)
 
     def finish(j):
-        whole, part = res.at[j, pl.ds(0, block)], res.at[j, pl.ds(0, block // 2)]
-        for m in range(3):
-            sent(j, 13 + m, res.at[j, pl.ds(0, cell)])
-        for message in (17, 18, 21, 22, 23, 24):
-            sent(j, message, whole)
-
-        def _passed():
-            sent(j, 19, part)
-            sent(j, 20, part)
-
-        either(j, lambda: sent(j, 19, whole), _passed)
-        theirs = other * half
-        for message, by in ((21, 0), (22, -1), (23, 1), (24, 2)):
-            got(j, message, piece_rows(j, theirs + step(p2, by) * block, block))
+        got(j, HALF, piece_rows(j, other * half, half))
+        sent(j, HALF, res.at[j, pl.ds(0, 3 * cell + 3 * block + half)])
 
     stages = {
         "own_half": own_half, "mid_1": mid_1, "sum_1": sum_1, "sum_2": sum_2, "gather_1": gather_1,
@@ -362,8 +338,8 @@
                 pltpu.VMEM((pieces, 3 * cell, width), bf16),
                 pltpu.SemaphoreType.DMA((matrices, 2)),
                 pltpu.SemaphoreType.DMA((pieces,)),
-                pltpu.SemaphoreType.DMA((pieces, MESSAGES)),
-                pltpu.SemaphoreType.DMA((pieces, MESSAGES)),
+                pltpu.SemaphoreType.DMA((pieces, HALF + 1)),
+                pltpu.SemaphoreType.DMA((pieces, HALF + 1)),
             ],
             compiler_params=pltpu.CompilerParams(
                 collective_id=0, has_side_effects=True, vmem_limit_bytes=VMEM_BYTES

time: 102 us -> 96.8 us (0.949)
  Pallas kernels: 101 us -> 96.7 us
    pallas_call x1, Pallas kernels: 97.5 us -> 92.7 us  [sums(): pl.pallas_call(functools.partial(kernel, pieces, width), out_shape=pltpu....]
where the time goes in v3:
time: 96.8 us; the launch traced here: 96.7 us
  Pallas kernels  96.7 us (100%)
    pallas_call x1, Pallas kernels, sums(): pl.pallas_call(functools.partial(kernel, pieces, width), out_shape=pltpu....  92.7 us
    pallas_call x1, Pallas kernels, sums(): pl.pallas_call(functools.partial(lay_out, pieces, width), out_shape=jax.S...  4.02 us

profile of v3, /device:TPU:97, one launch (start us, length us, event | category | flops | bytes accessed | tf_op | source)
XLA Modules:
  0.0 96.7 jit_solution(5424696328431784968)
XLA Ops:
  0.0 92.7 %shard_map.28.res = bf16[10,1024,512]{2,1,0:T(8,128)(2,1)S(1)} custom-call(bf16[1,2,4096,1024]{3,2,1,0:T(8,128)(2,1)} %a_hbm.1, bf16[1,2,4096,2560]{3,2,1,0:T(8,128)(2,1)} %g_hbm.1), custom_call_target="tpu_custom_call" | custom-call | tf_op jit(solution)/shard_map/pallas_call | solution.py:323
  92.7 4.0 %shard_map.29 = bf16[2,1024,2560]{2,1,0:T(8,128)(2,1)} custom-call(bf16[10,1024,512]{2,1,0:T(8,128)(2,1)S(1)} %shard_map.28.res), custom_call_target="tpu_custom_call" | custom-call | tf_op jit(solution)/shard_map/pallas_call | solution.py:348

commit v4 on v3

--- a/solution.py
+++ b/solution.py
@@ -35,7 +35,7 @@
 def kernel(
     pieces, width, a_hbm, g_hbm, res,
     a_buf, g_buf, own, pair_send, pair_recv, raw, mid1, sum1, recv1, recv2,
-    a_sem, g_sem, send_sem, recv_sem,
+    a_sem, g_sem, first_sem, send_sem, recv_sem,
 ):
     matrices, tokens, d = a_hbm.shape[1:]
     half = d // CORES
@@ -93,15 +93,27 @@
             g_hbm.at[0, n, :, pl.ds(pl.multiple_of(c * width, width), width)], g_buf.at[s], g_sem.at[j]
         )
 
-    def dot(j, h):
+    some = tokens // 2
+
+    def first_loads(k):
+        part = pl.ds(k * some, some)
+        columns = pl.ds(pl.multiple_of(other * half, half), half)
+        return (
+            pltpu.make_async_copy(a_hbm.at[0, 0, part, columns], a_buf.at[0, 0, part], first_sem.at[2 * k]),
+            pltpu.make_async_copy(g_hbm.at[0, 0, part, pl.ds(0, width)], g_buf.at[0, part], first_sem.at[2 * k + 1]),
+        )
+
+    def dot(j, h, first=0, count=tokens):
         n, s = j // per_matrix, lax.rem(j, G_SLOTS)
+        part = pl.ds(first, count)
         return lax.dot_general(
-            a_buf[n, h], g_buf[s], (((0,), (0,)), ((), ())), preferred_element_type=jnp.float32
+            a_buf[n, h, part], g_buf[s, part], (((0,), (0,)), ((), ())), preferred_element_type=jnp.float32
         )
 
     barrier = pltpu.get_barrier_semaphore()
-    load_a(0, 0).start()
-    load_g(0).start()
+    for k in range(2):
+        for load in first_loads(k):
+            load.start()
     for peer in peers:
         pl.semaphore_signal(barrier, inc=1, device_id={"dp": peer}, device_id_type=MESH)
     load_a(0, 1).start()
@@ -114,9 +126,14 @@
     def partner_send(j):
         send(j, PAIR, PAIR, pair_send.at[lax.rem(j, 2)], pair_recv.at[j], partner)
 
-    load_g(0).wait()
-    load_a(0, 0).wait()
-    partner_dot(0)
+    for k in range(2):
+        for load in first_loads(k):
+            load.wait()
+        value = dot(0, 0, k * some, some)
+        if k == 0:
+            own[0] = value
+        else:
+            pair_send[0] = (own[0] + value).astype(jnp.bfloat16)
     pl.semaphore_wait(barrier, len(peers))
     partner_send(0)
 
@@ -338,6 +355,7 @@
                 pltpu.VMEM((pieces, 3 * cell, width), bf16),
                 pltpu.SemaphoreType.DMA((matrices, 2)),
                 pltpu.SemaphoreType.DMA((pieces,)),
+                pltpu.SemaphoreType.DMA((4,)),
                 pltpu.SemaphoreType.DMA((pieces, HALF + 1)),
                 pltpu.SemaphoreType.DMA((pieces, HALF + 1)),
             ],

time: 96.8 us -> 95.7 us (0.989)
  Pallas kernels: 96.7 us -> 95.7 us
    pallas_call x1, Pallas kernels: 92.7 us -> 91.6 us  [sums(): pl.pallas_call(functools.partial(kernel, pieces, width), out_shape=pltpu....]
where the time goes in v4:
time: 95.7 us
  Pallas kernels  95.7 us (100%)
    pallas_call x1, Pallas kernels, sums(): pl.pallas_call(functools.partial(kernel, pieces, width), out_shape=pltpu....  91.6 us
    pallas_call x1, Pallas kernels, sums(): pl.pallas_call(functools.partial(lay_out, pieces, width), out_shape=jax.S...  4.02 us

profile of v4, /device:TPU:97, one launch (start us, length us, event | category | flops | bytes accessed | tf_op | source)
XLA Modules:
  0.0 95.7 jit_solution(1073366393105824049)
XLA Ops:
  0.0 91.6 %shard_map.28.res = bf16[10,1024,512]{2,1,0:T(8,128)(2,1)S(1)} custom-call(bf16[1,2,4096,1024]{3,2,1,0:T(8,128)(2,1)} %a_hbm.1, bf16[1,2,4096,2560]{3,2,1,0:T(8,128)(2,1)} %g_hbm.1), custom_call_target="tpu_custom_call" | custom-call | tf_op jit(solution)/shard_map/pallas_call | solution.py:340
  91.6 4.0 %shard_map.29 = bf16[2,1024,2560]{2,1,0:T(8,128)(2,1)} custom-call(bf16[10,1024,512]{2,1,0:T(8,128)(2,1)S(1)} %shard_map.28.res), custom_call_target="tpu_custom_call" | custom-call | tf_op jit(solution)/shard_map/pallas_call | solution.py:366
